TPU v7x, 32 devices: a whole 2x2x4 slice. The times are simulated.
32 devices in a mesh: cells: 8 (over z, x), genes: 4 (over y, core).
Axes of the slice: x: 2, y: 2, z: 4, core: 2. Of those that a mesh axis runs over, the one named last changes fastest.
Arguments:
- counts: int32 [38912, 4000], P('cells', 'genes'), may hold values from 0 to 674, as said below
- sketch: bfloat16 [4000, 128], P('genes'), may hold values from -6 to 6
Outputs:
- basis: float32 [38912, 128], P('cells')
- loadings: float32 [4000, 128], P('genes')
Inputs may be any that keep to these rules, and one draw needn't show every extreme that they name: `counts`: every cell and every gene has a positive total.
All inputs are finite; a program needn't handle non-finite values.
Results may differ from a plain program's by a relative error of at most 0.0051.
Values may be sent and summed in bfloat16 or wider, within the bound.
A program may use at most 128 MiB of HBM per device.

v0:
```python
import math

import jax
import jax.numpy as jnp
from jax import lax
from jax.sharding import PartitionSpec as P

ITERS = 2


def residual_block(block, cell_total, frac, limit):
    values = block.astype(jnp.float32)
    expected = cell_total[:, None] * frac[None, :]
    scaled = (values - expected) / jnp.sqrt(expected + 0.01 * expected * expected)
    return jnp.clip(scaled, -limit, limit).astype(jnp.bfloat16)


def self_gram(block):
    return lax.dot_general(
        block,
        block,
        (((0,), (0,)), ((), ())),
        precision=lax.Precision.HIGHEST,
        preferred_element_type=jnp.float32,
    )


def whitening(gram, count):
    width = gram.shape[0]
    identity = jnp.eye(width, dtype=jnp.float32)
    shifted = gram + 1e-05 * jnp.trace(gram) / width * identity
    lower = jnp.linalg.cholesky(shifted)
    inverse = jax.scipy.linalg.solve_triangular(lower, identity, lower=True)
    return jnp.transpose(inverse) * math.sqrt(count)


def transposed_product(left, right):
    return lax.dot_general(
        left, right, (((0,), (0,)), ((), ())), preferred_element_type=jnp.float32
    )


def loading_total(partial_sum, gene_scale):
    return lax.psum(partial_sum, "cells") * gene_scale


def shards(counts, sketch):
    cell_dev, gene_dev = counts.shape
    group_count = lax.axis_size("genes")
    cell_count = float(cell_dev * lax.axis_size("cells"))
    gene_count = float(gene_dev * group_count)
    cell_part = jnp.sum(counts, axis=1).astype(jnp.float32)
    gene_part = jnp.sum(counts, axis=0).astype(jnp.float32)
    gene_total, group_sum = lax.psum((gene_part, jnp.sum(gene_part)), "cells")
    cell_total, grand = lax.psum((cell_part, group_sum), "genes")
    frac = gene_total / grand
    limit = math.sqrt(cell_count)
    resid = residual_block(counts, cell_total, frac, limit)
    gene_scale = math.sqrt(gene_count) / cell_count
    omega = sketch
    basis = None
    loadings = None
    for sweep in range(ITERS):
        sketched = lax.psum(jnp.dot(resid, omega, preferred_element_type=jnp.float32), "genes")
        gram = lax.psum(self_gram(sketched), "cells")
        basis = jnp.dot(sketched, whitening(gram, cell_count), precision=lax.Precision.HIGHEST)
        partial_sum = transposed_product(resid, basis.astype(jnp.bfloat16))
        loadings = loading_total(partial_sum, gene_scale)
        if sweep < ITERS - 1:
            omega = loadings.astype(jnp.bfloat16)
    return (basis, loadings)


def solution(mesh):
    return jax.shard_map(
        shards,
        mesh=mesh,
        in_specs=(P("cells", "genes"), P("genes", None)),
        out_specs=(P("cells", None), P("genes", None)),
        check_vma=False,
    )
```

profile of v0, /device:TPU:0, one launch (start us, length us, event | category | flops | bytes accessed | tf_op | source)
XLA Modules:
  0.0 572.7 jit_solution(13577707791182518231)
XLA Ops:
  7.2 0.0 copy-start
  7.2 0.0 all-reduce.9.cloned.1.call-start
  7.2 8.2 %fusion.17 = (s32[4864]{0:T(1024)S(1)}, s32[1000]{0:T(1024)S(1)}) fusion(s32[4864,1000]{0,1:T(8,128)} %param.5), kind=kLoop, calls=%fused_computation.43 | loop fusion | flops 9722136 | bytes 19479456 | tf_op jit(solution)/shard_map/reduce_sum | solution.py:52
  15.4 0.6 convert_reduce_fusion
  16.0 24.0 %all-reduce = (f32[1000]{0:T(1024)S(1)}, f32[]{:T(128)}) all-reduce(f32[1000]{0:T(1024)S(1)} %convert_element_type.29, f32[]{:T(128)} %convert_reduce_fusion), channel_id=1, replica_groups=mesh['cells'=8,'genes'=4] {'cells'}, use_global_device_ids=true, to_apply=%region_3.0 | all-reduce | flops 1001 | bytes 8008 | tf_op jit(solution)/shard_map/psum | solution.py:54
  40.0 11.3 %all-reduce.1 = (f32[]{:T(128)}, f32[4864]{0:T(1024)S(1)}) all-reduce(f32[]{:T(128)} %get-tuple-element.7, f32[4864]{0:T(1024)S(1)} %convert_element_type.28), channel_id=1, replica_groups=mesh['cells'=8,'genes'=4] {'genes'}, use_global_device_ids=true, to_apply=%region_6.0 | all-reduce | flops 4865 | bytes 38920 | tf_op jit(solution)/shard_map/psum | solution.py:55
  51.3 0.6 broadcast_divide_fusion
  51.9 10.2 %fusion.2 = bf16[4864,1000]{0,1:T(8,128)(2,1)S(1)} fusion(s32[4864,1000]{0,1:T(8,128)} %param.5, f32[1000]{0:T(1024)S(1)} %broadcast_divide_fusion, f32[4864]{0:T(1024)S(1)} %get-tuple-element.9), kind=kLoop, calls=%fused_computation.6 | loop fusion | flops 43776000 | bytes 29207456 | tf_op jit(solution)/shard_map/convert_element_type | solution.py:15
  62.1 0.0 copy-start.1
  62.1 3.7 copy-done.1
  65.9 0.0 copy-done
  65.9 4.5 fusion.18
  70.3 0.0 all-reduce.9.cloned.1.call-update
  70.4 0.0 all-reduce.11.cloned.1.call-start
  70.4 54.2 %all-reduce.9.cloned.1.call-done = f32[4864,128]{1,0:T(8,128)} async-done(((f32[4864,128]{1,0:T(8,128)}), f32[4864,128]{1,0:T(8,128)}) %all-reduce.9.cloned.1.call-update) | async-done | bytes 2490384 | tf_op jit(solution)/shard_map/psum | solution.py:64
  124.6 0.0 copy-start.3
  124.6 7.3 %fusion.19 = f32[128,128]{0,1:T(8,128)} fusion(f32[4864,128]{1,0:T(8,128)} %all-reduce.9.cloned.1.call-done), kind=kOutput, calls=%fused_computation.45 | convolution fusion | flops 956301312 | bytes 2555904 | tf_op jit(solution)/shard_map/dot_general | solution.py:19
  131.9 0.0 all-reduce.11.cloned.1.call-update
  131.9 0.2 all-reduce.13.cloned.1.call-start
  132.1 69.3 %all-reduce.11.cloned.1.call-done = f32[128,128]{0,1:T(8,128)} async-done(((f32[128,128]{0,1:T(8,128)}), f32[128,128]{0,1:T(8,128)}) %all-reduce.11.cloned.1.call-update) | async-done | bytes 65552 | tf_op jit(solution)/shard_map/psum | solution.py:65
  201.4 1.5 select_reduce_fusion.3
  203.5 0.9 select_add_fusion.1
  204.4 0.1 copy.5
  204.5 0.9 fusion.15
  205.3 11.7 %cholesky.44 = f32[128,128]{1,0:T(8,128)S(1)} custom-call(f32[128,128]{1,0:T(8,128)S(1)} %fusion.15), custom_call_target="Cholesky" | custom-call | tf_op jit(solution)/shard_map/jit(cholesky)/cholesky | solution.py:32
  217.1 0.6 compare_reduce_fusion.1
  217.7 0.7 fusion.10
  218.4 9.8 %custom-call.6 = f32[1,128,128]{1,2,0:T(8,128)S(1)} custom-call(f32[1,128,128]{2,1,0:T(8,128)S(1)} %fusion.10), custom_call_target="InvertDiagBlocksLowerTriangular" | custom-call | tf_op jit(solution)/shard_map/jit(_solve_triangular)/triangular_solve | solution.py:33
  228.2 0.3 convolution_multiply_fusion.1
  228.5 0.0 copy-done.3
  228.5 2.1 convolution_convert_fusion
  230.6 7.3 %fusion.20 = f32[1000,128]{1,0:T(8,128)} fusion(bf16[4864,1000]{0,1:T(8,128)(2,1)} %copy-done.1, bf16[4864,128]{1,0:T(8,128)(2,1)S(1)} %convolution_convert_fusion), kind=kOutput, calls=%fused_computation.46 | convolution fusion | flops 1245184000 | bytes 11485184 | tf_op jit(solution)/shard_map/dot_general | solution.py:38
  237.9 0.0 all-reduce.13.cloned.1.call-update
  237.9 0.3 all-reduce.15.cloned.1.call-start
  238.2 72.4 %all-reduce.13.cloned.1.call-done = f32[1000,128]{1,0:T(8,128)} async-done(((f32[1000,128]{1,0:T(8,128)}), f32[1000,128]{1,0:T(8,128)}) %all-reduce.13.cloned.1.call-update) | async-done | bytes 512016 | tf_op jit(solution)/shard_map/psum | solution.py:44
  310.6 8.1 %fusion.6 = f32[4864,128]{1,0:T(8,128)} fusion(bf16[4864,1000]{0,1:T(8,128)(2,1)} %copy-done.1, f32[1000,128]{1,0:T(8,128)} %all-reduce.13.cloned.1.call-done), kind=kOutput, calls=%fused_computation.14 | convolution fusion | flops 1245440000 | bytes 12730368 | tf_op jit(solution)/shard_map/dot_general | solution.py:64
  318.7 0.0 all-reduce.15.cloned.1.call-update
  318.8 0.0 all-reduce.17.cloned.1.call-start
  318.8 57.2 %all-reduce.15.cloned.1.call-done = f32[4864,128]{1,0:T(8,128)} async-done(((f32[4864,128]{1,0:T(8,128)}), f32[4864,128]{1,0:T(8,128)}) %all-reduce.15.cloned.1.call-update) | async-done | bytes 2490384 | tf_op jit(solution)/shard_map/psum | solution.py:64
  376.0 0.0 copy-start.2
  376.0 7.3 %fusion.21 = f32[128,128]{0,1:T(8,128)} fusion(f32[4864,128]{1,0:T(8,128)} %all-reduce.15.cloned.1.call-done), kind=kOutput, calls=%fused_computation.47 | convolution fusion | flops 956301312 | bytes 2555904 | tf_op jit(solution)/shard_map/dot_general | solution.py:19
  383.3 0.0 all-reduce.17.cloned.1.call-update
  383.3 0.3 all-reduce.19.cloned.1.call-start
  383.6 69.2 %all-reduce.17.cloned.1.call-done = f32[128,128]{0,1:T(8,128)} async-done(((f32[128,128]{0,1:T(8,128)}), f32[128,128]{0,1:T(8,128)}) %all-reduce.17.cloned.1.call-update) | async-done | bytes 65552 | tf_op jit(solution)/shard_map/psum | solution.py:65
  452.8 1.5 select_reduce_fusion.2
  454.9 0.9 select_add_fusion
  455.8 0.1 copy.7
  455.9 0.9 fusion.13
  456.7 11.7 %cholesky.55 = f32[128,128]{1,0:T(8,128)S(1)} custom-call(f32[128,128]{1,0:T(8,128)S(1)} %fusion.13), custom_call_target="Cholesky" | custom-call | tf_op jit(solution)/shard_map/jit(cholesky)/cholesky | solution.py:32
  468.5 0.6 compare_reduce_fusion
  469.1 0.7 fusion.11
  469.8 9.8 %custom-call.7 = f32[1,128,128]{1,2,0:T(8,128)S(1)} custom-call(f32[1,128,128]{2,1,0:T(8,128)S(1)} %fusion.11), custom_call_target="InvertDiagBlocksLowerTriangular" | custom-call | tf_op jit(solution)/shard_map/jit(_solve_triangular)/triangular_solve | solution.py:33
  479.6 0.3 convolution_multiply_fusion
  479.9 0.0 copy-done.2
  479.9 2.2 fusion.22
  482.1 0.0 copy-start.4
  482.1 1.4 copy-done.4
  483.6 7.3 %fusion.4 = f32[1000,128]{1,0:T(8,128)} fusion(bf16[4864,1000]{0,1:T(8,128)(2,1)} %copy-done.1, f32[4864,128]{1,0:T(8,128)S(1)} %fusion.22), kind=kOutput, calls=%fused_computation.9 | convolution fusion | flops 1245806592 | bytes 12730368 | tf_op jit(solution)/shard_map/dot_general | solution.py:38
  490.8 0.0 all-reduce.19.cloned.1.call-update
  490.9 72.7 %all-reduce.19.cloned.1.call-done = f32[1000,128]{1,0:T(8,128)} async-done(((f32[1000,128]{1,0:T(8,128)}), f32[1000,128]{1,0:T(8,128)}) %all-reduce.19.cloned.1.call-update) | async-done | bytes 512016 | tf_op jit(solution)/shard_map/psum | solution.py:44
  563.5 1.9 broadcast_multiply_fusion
  (4 shorter events, 0.1 us)
Async XLA Ops:
  7.2 58.7 %copy-start = (bf16[1000,128]{1,0:T(8,128)(2,1)S(1)}, bf16[1000,128]{1,0:T(8,128)(2,1)}, u32[]{:S(2)}) copy-start(bf16[1000,128]{1,0:T(8,128)(2,1)} %param.6) | copy-start | bytes 768004
  7.2 117.4 %all-reduce.9.cloned.1.call-start = ((), (), s32[]{:S(2)}) async-start(), calls=%async_computation | async-start | bytes 4980736 | tf_op jit(solution)/shard_map/psum | solution.py:64
  62.1 3.7 copy-start.1
  70.4 131.0 %all-reduce.11.cloned.1.call-start = ((), (), s32[]{:S(2)}) async-start(), calls=%async_computation.1 | async-start | bytes 131072 | tf_op jit(solution)/shard_map/psum | solution.py:65
  124.6 103.9 %copy-start.3 = (f32[4864,128]{1,0:T(8,128)S(1)}, f32[4864,128]{1,0:T(8,128)}, u32[]{:S(2)}) copy-start(f32[4864,128]{1,0:T(8,128)} %all-reduce.9.cloned.1.call-done) | copy-start | bytes 7471108
  131.9 178.7 %all-reduce.13.cloned.1.call-start = ((), (), s32[]{:S(2)}) async-start(), calls=%async_computation.2 | async-start | bytes 1024000 | tf_op jit(solution)/shard_map/psum | solution.py:44
  237.9 138.0 %all-reduce.15.cloned.1.call-start = ((), (), s32[]{:S(2)}) async-start(), calls=%async_computation.3 | async-start | bytes 4980736 | tf_op jit(solution)/shard_map/psum | solution.py:64
  318.8 134.0 %all-reduce.17.cloned.1.call-start = ((), (), s32[]{:S(2)}) async-start(), calls=%async_computation.4 | async-start | bytes 131072 | tf_op jit(solution)/shard_map/psum | solution.py:65
  376.0 103.9 %copy-start.2 = (f32[4864,128]{1,0:T(8,128)S(1)}, f32[4864,128]{1,0:T(8,128)}, u32[]{:S(2)}) copy-start(f32[4864,128]{1,0:T(8,128)} %all-reduce.15.cloned.1.call-done) | copy-start | bytes 7471108
  383.3 180.2 %all-reduce.19.cloned.1.call-start = ((), (), s32[]{:S(2)}) async-start(), calls=%async_computation.5 | async-start | bytes 1024000 | tf_op jit(solution)/shard_map/psum | solution.py:44
  482.1 1.5 copy-start.4
Sparse Core Ops, SparseCore 0:
  70.5 54.0 all-reduce.8
  132.0 69.3 all-reduce.10
  238.1 72.5 all-reduce.12
  318.9 57.0 all-reduce.14
  383.4 69.3 all-reduce.16
  491.0 72.5 all-reduce.18
where the time goes:
time: 581 us; the launch traced here: 573 us
  waiting for transfers between devices  395 us (68%)
  other arithmetic  73.6 us (13%)
  matrix products  46.6 us (8%)
  blocking collectives  35.3 us (6%)
  between operations  16 us (3%)
    psum x2, waiting for transfers between devices, loading_total(): return lax.psum(partial_sum, 'cells') * gene_scale  145 us
    psum x2, waiting for transfers between devices, shards(): gram = lax.psum(self_gram(sketched), 'cells')  138 us
    psum x2, waiting for transfers between devices, shards(): lax.psum(jnp.dot(resid, omega, preferred_element_type=jnp.float32), 'genes')  111 us
    another operation x6, other arithmetic, whitening(): lower = jnp.linalg.cholesky(shifted)  24.8 us
    psum x1, blocking collectives, shards(): gene_total, group_sum = lax.psum((gene_part, jnp.sum(gene_part)), 'cells')  24 us
    another operation x4, other arithmetic, whitening(): inverse = jax.scipy.linalg.solve_triangular(lower, identity, lower=True)  20.9 us
    dot_general x2, matrix products, self_gram(): lax.dot_general(block, block, (((0,), (0,)), ((), ())), precision=lax.Pre...  14.6 us
    dot_general x2, matrix products, transposed_product(): lax.dot_general(left, right, (((0,), (0,)), ((), ())), preferred_element_...  14.6 us
  transfers between devices with their start and end apart: 6, of which 6 were waited for; matrix products, arithmetic and copies ran while one was open for 0% of the time, Pallas kernels for 0%

commit v1 on v0

v1 whole, which is shorter than its diff:
```python
import functools
import math

import jax
import jax.numpy as jnp
from jax import lax
from jax.experimental import pallas as pl
from jax.experimental.pallas import tpu as pltpu
from jax.sharding import PartitionSpec as P

ITERS = 2
MESH = pl.DeviceIdType.MESH


def greet(peers):
    barrier = pltpu.get_barrier_semaphore()
    for peer in peers:
        pl.semaphore_signal(barrier, inc=1, device_id=peer, device_id_type=MESH)
    pl.semaphore_wait(barrier, len(peers))


def ring_peers(axis, count):
    me = lax.axis_index(axis)
    return [{axis: lax.rem(me + step, count)} for step in range(1, count)]


def send(src, dst, sems, slot, peer):
    copy = pltpu.make_async_remote_copy(
        src_ref=src,
        dst_ref=dst,
        send_sem=sems.at[0, slot],
        recv_sem=sems.at[1, slot],
        device_id=peer,
        device_id_type=MESH,
    )
    copy.start()
    return copy


def sems(count):
    return pltpu.SemaphoreType.DMA((2, max(count, 1)))


def remote_call(body, out_shape, scratch, ident):
    leaves = jax.tree.leaves(out_shape)
    specs = [pl.BlockSpec(memory_space=pltpu.VMEM)] * len(leaves)

    def call(*args):
        return pl.pallas_call(
            body,
            out_shape=out_shape,
            in_specs=[pl.BlockSpec(memory_space=pltpu.VMEM)] * len(args),
            out_specs=specs if isinstance(out_shape, (list, tuple)) else specs[0],
            scratch_shapes=scratch,
            compiler_params=pltpu.CompilerParams(
                collective_id=ident, has_side_effects=True, vmem_limit_bytes=16 * 1024 * 1024
            ),
        )(*args)

    return call


def totals_body(n, m, gene_ref, cell_ref, gene_out, cell_out, grand_out, gene_buf, cell_buf, row, row_buf, gene_sem, cell_sem, row_sem):
    cell_peers = ring_peers("cells", n)
    gene_peers = ring_peers("genes", m)
    greet(cell_peers + gene_peers)
    gene_copies = [send(gene_ref, gene_buf.at[i], gene_sem, i, peer) for i, peer in enumerate(cell_peers)]
    cell_copies = [send(cell_ref, cell_buf.at[i], cell_sem, i, peer) for i, peer in enumerate(gene_peers)]
    total = gene_ref[...]
    for i, copy in enumerate(gene_copies):
        copy.wait_recv()
        total = total + gene_buf[i]
    gene_out[...] = total
    row[...] = jnp.broadcast_to(jnp.sum(total, axis=0, keepdims=True), row.shape)
    row_copies = [send(row, row_buf.at[i], row_sem, i, peer) for i, peer in enumerate(gene_peers)]
    total = cell_ref[...]
    for i, copy in enumerate(cell_copies):
        copy.wait_recv()
        total = total + cell_buf[i]
    cell_out[...] = total
    total = row[...]
    for i, copy in enumerate(row_copies):
        copy.wait_recv()
        total = total + row_buf[i]
    grand_out[...] = total
    for copy in gene_copies + cell_copies + row_copies:
        copy.wait_send()


def all_totals(gene_part, cell_part, n, m, ident):
    f32 = jnp.float32
    return remote_call(
        functools.partial(totals_body, n, m),
        [
            jax.ShapeDtypeStruct(gene_part.shape, f32),
            jax.ShapeDtypeStruct(cell_part.shape, f32),
            jax.ShapeDtypeStruct((8, 128), f32),
        ],
        [
            pltpu.VMEM((n - 1,) + gene_part.shape, f32),
            pltpu.VMEM((m - 1,) + cell_part.shape, f32),
            pltpu.VMEM((8, 128), f32),
            pltpu.VMEM((m - 1, 8, 128), f32),
            sems(n - 1),
            sems(m - 1),
            sems(m - 1),
        ],
        ident,
    )(gene_part, cell_part)


def gene_places(m):
    me = lax.axis_index("genes")
    rows = m // 2
    core, row = lax.rem(me, 2), lax.div(me, 2)
    partner = {"genes": row * 2 + 1 - core}
    others = [lax.rem(row + step, rows) for step in range(1, rows)]
    return core, row, partner, others, [{"genes": other * 2 + core} for other in others]


def scatter_body(m, x_ref, out_ref, near, outgoing, far, near_sem, far_sem):
    core, row, partner, others, peers = gene_places(m)
    greet([partner] + peers)
    first = [send(x_ref.at[1 - core, other], near.at[other], near_sem, i, partner) for i, other in enumerate(others + [row])]
    second = []
    for i, other in enumerate(others):
        first[i].wait_recv()
        outgoing[i] = x_ref[core, other] + near[other]
        second.append(send(outgoing.at[i], far.at[i], far_sem, i, peers[i]))
    first[-1].wait_recv()
    out_ref[...] = x_ref[core, row] + near[row]
    for i, copy in enumerate(second):
        copy.wait_recv()
        out_ref[...] += far[i]
    for copy in first + second:
        copy.wait_send()


def scatter_genes(x, m, ident):
    block = x.shape[0] // m
    rows = m // 2
    f32 = jnp.float32
    return remote_call(
        functools.partial(scatter_body, m),
        jax.ShapeDtypeStruct((block, x.shape[1]), f32),
        [
            pltpu.VMEM((rows, block, x.shape[1]), f32),
            pltpu.VMEM((max(rows - 1, 1), block, x.shape[1]), f32),
            pltpu.VMEM((max(rows - 1, 1), block, x.shape[1]), f32),
            sems(rows),
            sems(rows - 1),
        ],
        ident,
    )(x.reshape(2, rows, block, x.shape[1]))


def gather_body(m, x_ref, out_ref, far_sem, near_sem):
    core, row, partner, others, peers = gene_places(m)
    rows = m // 2
    greet([partner] + peers)
    mine = out_ref.at[core, row]
    out_ref[core, row] = x_ref[...]
    far = [send(x_ref, mine, far_sem, i, peer) for i, peer in enumerate(peers)]
    near = [send(x_ref, mine, near_sem, 0, partner)]
    for i in range(rows - 1):
        far[i].wait_recv()
        origin = lax.rem(row + rows - 1 - i, rows)
        near.append(send(out_ref.at[core, origin], out_ref.at[core, origin], near_sem, i + 1, partner))
    for copy in near:
        copy.wait_recv()
    for copy in far + near:
        copy.wait_send()


def gather_genes(x, m, ident):
    rows = m // 2
    out = remote_call(
        functools.partial(gather_body, m),
        jax.ShapeDtypeStruct((2, rows) + x.shape, x.dtype),
        [sems(rows - 1), sems(rows)],
        ident,
    )(x)
    return out.reshape(m * x.shape[0], x.shape[1])


def gram_body(n, m, x_ref, out_ref, buf, part, part_buf, first_sem, part_sem, last_sem):
    me = lax.axis_index("cells")
    cell_peers = ring_peers("cells", n)
    gene_peers = ring_peers("genes", m)
    greet(cell_peers + gene_peers)
    first = [send(x_ref.at[peer["cells"]], buf.at[i], first_sem, i, peer) for i, peer in enumerate(cell_peers)]
    total = x_ref[me]
    for i, copy in enumerate(first):
        copy.wait_recv()
        total = total + buf[i]
    part[...] = total
    middle = [send(part, part_buf.at[i], part_sem, i, peer) for i, peer in enumerate(gene_peers)]
    for i, copy in enumerate(middle):
        copy.wait_recv()
        total = total + part_buf[i]
    out_ref[me] = total
    last = [send(out_ref.at[me], out_ref.at[me], last_sem, i, peer) for i, peer in enumerate(cell_peers)]
    for copy in last:
        copy.wait_recv()
    for copy in first + middle + last:
        copy.wait_send()


def sum_gram(gram, n, m, ident):
    width = gram.shape[0]
    shape = (n, width // n, width)
    f32 = jnp.float32
    out = remote_call(
        functools.partial(gram_body, n, m),
        jax.ShapeDtypeStruct(shape, f32),
        [
            pltpu.VMEM((n - 1,) + shape[1:], f32),
            pltpu.VMEM(shape[1:], f32),
            pltpu.VMEM((m - 1,) + shape[1:], f32),
            sems(n - 1),
            sems(m - 1),
            sems(n - 1),
        ],
        ident,
    )(gram.reshape(shape))
    return out.reshape(width, width)


def loading_body(n, scale, x_ref, out_ref, buf, first_sem, last_sem):
    me = lax.axis_index("cells")
    peers = ring_peers("cells", n)
    greet(peers)
    first = [send(x_ref.at[peer["cells"]], buf.at[i], first_sem, i, peer) for i, peer in enumerate(peers)]
    total = x_ref[me]
    for i, copy in enumerate(first):
        copy.wait_recv()
        total = total + buf[i]
    out_ref[me] = (total * scale).astype(out_ref.dtype)
    last = [send(out_ref.at[me], out_ref.at[me], last_sem, i, peer) for i, peer in enumerate(peers)]
    for copy in last:
        copy.wait_recv()
    for copy in first + last:
        copy.wait_send()


def loading_total(partial_sum, scale, n, ident):
    genes, width = partial_sum.shape
    unit = 16 * n
    padded = -(-genes // unit) * unit
    shape = (n, padded // n, width)
    x = jnp.pad(partial_sum, ((0, padded - genes), (0, 0))).reshape(shape)
    out = remote_call(
        functools.partial(loading_body, n, scale),
        jax.ShapeDtypeStruct(shape, jnp.bfloat16),
        [pltpu.VMEM((n - 1,) + shape[1:], jnp.float32), sems(n - 1), sems(n - 1)],
        ident,
    )(x)
    return out.reshape(padded, width)[:genes]


def residual_block(block, cell_total, frac, limit):
    values = block.astype(jnp.float32)
    expected = cell_total[:, None] * frac[None, :]
    scaled = (values - expected) / jnp.sqrt(expected + 0.01 * expected * expected)
    return jnp.clip(scaled, -limit, limit).astype(jnp.bfloat16)


def self_gram(block):
    return lax.dot_general(
        block,
        block,
        (((0,), (0,)), ((), ())),
        precision=lax.Precision.HIGHEST,
        preferred_element_type=jnp.float32,
    )


def whitening(gram, count):
    width = gram.shape[0]
    identity = jnp.eye(width, dtype=jnp.float32)
    shifted = gram + 1e-05 * jnp.trace(gram) / width * identity
    lower = jnp.linalg.cholesky(shifted)
    inverse = jax.scipy.linalg.solve_triangular(lower, identity, lower=True)
    return jnp.transpose(inverse) * math.sqrt(count)


def transposed_product(left, right):
    return lax.dot_general(
        left, right, (((0,), (0,)), ((), ())), preferred_element_type=jnp.float32
    )


def as_rows(vector):
    length = vector.shape[0]
    padded = -(-length // 128) * 128
    return jnp.pad(vector, (0, padded - length)).reshape(padded // 128, 128)


def shards(counts, sketch):
    cell_dev, gene_dev = counts.shape
    n, m = lax.axis_size("cells"), lax.axis_size("genes")
    cell_count = float(cell_dev * n)
    gene_count = float(gene_dev * m)
    cell_part = jnp.sum(counts, axis=1).astype(jnp.float32)
    gene_part = jnp.sum(counts, axis=0).astype(jnp.float32)
    gene_rows, cell_rows, grand_rows = all_totals(as_rows(gene_part), as_rows(cell_part), n, m, 0)
    gene_total = gene_rows.reshape(-1)[:gene_dev]
    cell_total = cell_rows.reshape(-1)[:cell_dev]
    frac = gene_total / jnp.sum(grand_rows[0])
    limit = math.sqrt(cell_count)
    resid = residual_block(counts, cell_total, frac, limit)
    gene_scale = math.sqrt(gene_count) / cell_count
    omega = sketch
    basis = None
    for sweep in range(ITERS):
        ident = 1 + 4 * sweep
        part = jnp.dot(resid, omega, preferred_element_type=jnp.float32)
        own = scatter_genes(part, m, ident)
        gram = sum_gram(self_gram(own), n, m, ident + 1)
        own_basis = jnp.dot(own, whitening(gram, cell_count), precision=lax.Precision.HIGHEST)
        basis = gather_genes(own_basis.astype(jnp.bfloat16), m, ident + 2)
        partial_sum = transposed_product(resid, basis)
        omega = loading_total(partial_sum, gene_scale, n, ident + 3)
    return (basis.astype(jnp.float32), omega.astype(jnp.float32))


def solution(mesh):
    return jax.shard_map(
        shards,
        mesh=mesh,
        in_specs=(P("cells", "genes"), P("genes", None)),
        out_specs=(P("cells", None), P("genes", None)),
        check_vma=False,
    )
```

time: 581 us -> 238 us (0.41); the launches traced: 573 us -> 238 us
  waiting for transfers between devices: 395 us -> 0 us
  Pallas kernels: 0 us -> 144 us
  blocking collectives: 35.3 us -> 0 us
  matrix products: 46.6 us -> 21.3 us
  between operations: 16 us -> 2.27 us
    psum x6 -> x0, waiting for transfers between devices: 395 us -> none  [the longest x2 145 us: loading_total(): return lax.psum(partial_sum, 'cells') * gene_scale]
    pallas_call x0 -> x9, Pallas kernels: none -> 144 us  [call(): pl.pallas_call(body, out_shape=out_shape, in_specs=[pl.BlockSpec(memory_s...]
    psum x2 -> x0, blocking collectives: 35.3 us -> none  [the longest x1 24 us: shards(): gene_total, group_sum = lax.psum((gene_part, jnp.sum(gene_part)), 'cells')]
    dot_general x2, matrix products: 14.6 us -> 2.54 us  [self_gram(): lax.dot_general(block, block, (((0,), (0,)), ((), ())), precision=lax.Pre...]
    dot_general x4, matrix products: 16.9 us -> 7.14 us  [the longest x2 5.83 us: shards(): part = jnp.dot(resid, omega, preferred_element_type=jnp.float32)]
  transfers between devices with their start and end apart: 6 -> 0, of which waited for: 6 -> 0; matrix products, arithmetic and copies ran while one was open for 0% -> 0% of each run, Pallas kernels for 0% -> 0%
where the time goes in v1:
time: 238 us
  Pallas kernels  144 us (61%)
  other arithmetic  69.4 us (29%)
  matrix products  21.3 us (9%)
    pallas_call x9, Pallas kernels, call(): pl.pallas_call(body, out_shape=out_shape, in_specs=[pl.BlockSpec(memory_s...  144 us
    another operation x6, other arithmetic, whitening(): lower = jnp.linalg.cholesky(shifted)  24.8 us
    another operation x4, other arithmetic, whitening(): inverse = jax.scipy.linalg.solve_triangular(lower, identity, lower=True)  20.9 us
    dot_general x2, matrix products, transposed_product(): lax.dot_general(left, right, (((0,), (0,)), ((), ())), preferred_element_...  11.1 us
    convert_element_type x1, other arithmetic, residual_block(): return jnp.clip(scaled, -limit, limit).astype(jnp.bfloat16)  10.4 us
    reduce_sum x1, other arithmetic, shards(): cell_part = jnp.sum(counts, axis=1).astype(jnp.float32)  8.15 us
    dot_general x2, matrix products, shards(): part = jnp.dot(resid, omega, preferred_element_type=jnp.float32)  5.83 us

profile of v1, /device:TPU:0, one launch (start us, length us, event | category | flops | bytes accessed | tf_op | source)
XLA Modules:
  0.0 237.7 jit_solution(396012188322631643)
XLA Ops:
  0.6 0.0 copy-start
  0.7 8.2 %fusion.14 = (s32[4864]{0:T(1024)S(1)}, s32[1000]{0:T(1024)S(1)}) fusion(s32[4864,1000]{0,1:T(8,128)} %param.5), kind=kLoop, calls=%fused_computation.45 | loop fusion | flops 9722136 | bytes 19479456 | tf_op jit(solution)/shard_map/reduce_sum | solution.py:304
  8.8 11.8 %shard_map.41 = (f32[8,128]{1,0:T(8,128)S(1)}, f32[38,128]{1,0:T(8,128)S(1)}, f32[8,128]{1,0:T(8,128)S(1)}) custom-call(f32[8,128]{1,0:T(8,128)S(1)} %pad_bitcast_fusion.gene_ref, f32[38,128]{1,0:T(8,128)S(1)} %convert_bitcast_fusion.cell_ref), custom_call_target="tpu_custom_call" | custom-call | tf_op jit(solution)/shard_map/pallas_call | solution.py:49
  20.6 0.6 slice_reduce_fusion
  21.2 0.6 slice_divide_fusion
  21.9 10.4 %fusion.2 = bf16[4864,1000]{0,1:T(8,128)(2,1)S(1)} fusion(s32[4864,1000]{0,1:T(8,128)} %param.5, f32[1000]{0:T(1024)S(1)} %slice_divide_fusion, f32[4864]{0:T(1024)S(1)} %bitcast.64), kind=kLoop, calls=%fused_computation.6 | loop fusion | flops 43776000 | bytes 29207456 | tf_op jit(solution)/shard_map/convert_element_type | solution.py:265
  32.2 0.0 copy-done
  32.3 0.0 copy-start.1
  32.3 2.9 %fusion.15 = f32[4864,128]{1,0:T(8,128)S(1)} fusion(bf16[4864,1000]{0,1:T(8,128)(2,1)S(1)} %fusion.2, bf16[1000,128]{1,0:T(8,128)(2,1)S(1)} %copy-done), kind=kOutput, calls=%fused_computation.46 | convolution fusion | flops 1245184000 | bytes 12474368 | tf_op jit(solution)/shard_map/dot_general | solution.py:317
  35.2 18.6 %shard_map.42 = f32[1216,128]{1,0:T(8,128)S(1)} custom-call(f32[2,2,1216,128]{3,2,1,0:T(8,128)S(1)} %bitcast.53), custom_call_target="tpu_custom_call" | custom-call | tf_op jit(solution)/shard_map/pallas_call | solution.py:49
  53.8 1.3 fusion.16
  55.1 15.1 %shard_map.43 = f32[8,16,128]{2,1,0:T(8,128)S(1)} custom-call(f32[8,16,128]{2,1,0:T(8,128)S(1)} %bitcast.62), custom_call_target="tpu_custom_call" | custom-call | tf_op jit(solution)/shard_map/pallas_call | solution.py:49
  70.2 0.0 copy-done.1
  70.2 0.7 select_reduce_fusion.3
  71.5 0.1 copy.8
  71.7 0.1 copy.9
  71.8 11.7 %cholesky.44 = f32[128,128]{1,0:T(8,128)S(1)} custom-call(f32[128,128]{1,0:T(8,128)S(1)} %fusion.13), custom_call_target="Cholesky" | custom-call | tf_op jit(solution)/shard_map/jit(cholesky)/cholesky | solution.py:282
  83.5 0.6 compare_reduce_fusion.1
  84.2 0.7 fusion.8
  84.8 9.8 %custom-call.6 = f32[1,128,128]{1,2,0:T(8,128)S(1)} custom-call(f32[1,128,128]{2,1,0:T(8,128)S(1)} %fusion.8), custom_call_target="InvertDiagBlocksLowerTriangular" | custom-call | tf_op jit(solution)/shard_map/jit(_solve_triangular)/triangular_solve | solution.py:283
  94.6 0.0 copy-start.2
  94.7 0.3 convolution_multiply_fusion.1
  94.9 0.7 convolution_convert_fusion.1.x_ref
  95.6 10.9 %shard_map.44 = bf16[2,2,1216,128]{3,2,1,0:T(8,128)(2,1)S(1)} custom-call(bf16[1216,128]{1,0:T(8,128)(2,1)S(1)} %convolution_convert_fusion.1.x_ref), custom_call_target="tpu_custom_call" | custom-call | tf_op jit(solution)/shard_map/pallas_call | solution.py:49
  106.5 5.6 %fusion.17 = f32[1000,128]{1,0:T(8,128)S(1)} fusion(bf16[4864,1000]{0,1:T(8,128)(2,1)} %copy-done.1, bf16[4864,128]{1,0:T(8,128)(2,1)S(1)} %bitcast.57), kind=kOutput, calls=%fused_computation.48 | convolution fusion | flops 1245184000 | bytes 11485184 | tf_op jit(solution)/shard_map/dot_general | solution.py:288
  112.2 21.8 %shard_map.45 = bf16[8,128,128]{2,1,0:T(8,128)(2,1)S(1)} custom-call(f32[8,128,128]{2,1,0:T(8,128)S(1)} %bitcast.56), custom_call_target="tpu_custom_call" | custom-call | tf_op jit(solution)/shard_map/pallas_call | solution.py:49
  134.0 0.0 copy-done.2
  134.0 2.9 %fusion.4 = f32[4864,128]{1,0:T(8,128)S(1)} fusion(bf16[4864,1000]{0,1:T(8,128)(2,1)S(1)} %copy-done.2, bf16[1024,128]{1,0:T(8,128)(2,1)S(1)} %bitcast.59), kind=kOutput, calls=%fused_computation.13 | convolution fusion | flops 1245184000 | bytes 12474368 | tf_op jit(solution)/shard_map/dot_general | solution.py:317
  136.9 16.8 %shard_map.46 = f32[1216,128]{1,0:T(8,128)S(1)} custom-call(f32[2,2,1216,128]{3,2,1,0:T(8,128)S(1)} %bitcast.52), custom_call_target="tpu_custom_call" | custom-call | tf_op jit(solution)/shard_map/pallas_call | solution.py:49
  153.8 1.3 fusion.18
  155.1 15.4 %shard_map.47 = f32[8,16,128]{2,1,0:T(8,128)S(1)} custom-call(f32[8,16,128]{2,1,0:T(8,128)S(1)} %bitcast.63), custom_call_target="tpu_custom_call" | custom-call | tf_op jit(solution)/shard_map/pallas_call | solution.py:49
  170.5 0.7 select_reduce_fusion.2
  171.8 0.1 copy.10
  171.9 0.1 copy.11
  172.1 11.7 %cholesky.55 = f32[128,128]{1,0:T(8,128)S(1)} custom-call(f32[128,128]{1,0:T(8,128)S(1)} %fusion.11), custom_call_target="Cholesky" | custom-call | tf_op jit(solution)/shard_map/jit(cholesky)/cholesky | solution.py:282
  183.8 0.6 compare_reduce_fusion
  184.5 0.7 fusion.9
  185.1 9.8 %custom-call.7 = f32[1,128,128]{1,2,0:T(8,128)S(1)} custom-call(f32[1,128,128]{2,1,0:T(8,128)S(1)} %fusion.9), custom_call_target="InvertDiagBlocksLowerTriangular" | custom-call | tf_op jit(solution)/shard_map/jit(_solve_triangular)/triangular_solve | solution.py:283
  194.9 0.3 convolution_multiply_fusion
  195.2 0.7 convolution_convert_fusion.x_ref
  195.9 9.9 %shard_map.48 = bf16[2,2,1216,128]{3,2,1,0:T(8,128)(2,1)S(1)} custom-call(bf16[1216,128]{1,0:T(8,128)(2,1)S(1)} %convolution_convert_fusion.x_ref), custom_call_target="tpu_custom_call" | custom-call | tf_op jit(solution)/shard_map/pallas_call | solution.py:49
  205.8 5.4 %fusion.19 = f32[1000,128]{1,0:T(8,128)S(1)} fusion(bf16[4864,1000]{0,1:T(8,128)(2,1)} %copy-done.1, bf16[4864,128]{1,0:T(8,128)(2,1)S(1)} %bitcast.54), kind=kOutput, calls=%fused_computation.50 | convolution fusion | flops 1245184000 | bytes 11485184 | tf_op jit(solution)/shard_map/dot_general | solution.py:288
  211.3 23.9 %shard_map.49 = bf16[8,128,128]{2,1,0:T(8,128)(2,1)S(1)} custom-call(f32[8,128,128]{2,1,0:T(8,128)S(1)} %bitcast.55), custom_call_target="tpu_custom_call" | custom-call | tf_op jit(solution)/shard_map/pallas_call | solution.py:49
  235.2 0.8 slice_convert_fusion
  236.0 1.7 bitcast_convert_fusion
  (12 shorter events, 0.2 us)
Async XLA Ops:
  0.6 31.6 %copy-start = (bf16[1000,128]{1,0:T(8,128)(2,1)S(1)}, bf16[1000,128]{1,0:T(8,128)(2,1)}, u32[]{:S(2)}) copy-start(bf16[1000,128]{1,0:T(8,128)(2,1)} %param.6) | copy-start | bytes 768004
  32.3 37.9 %copy-start.1 = (bf16[4864,1000]{0,1:T(8,128)(2,1)}, bf16[4864,1000]{0,1:T(8,128)(2,1)S(1)}, u32[]{:S(2)}) copy-start(bf16[4864,1000]{0,1:T(8,128)(2,1)S(1)} %fusion.2) | copy-start | bytes 29184004
  94.6 39.4 %copy-start.2 = (bf16[4864,1000]{0,1:T(8,128)(2,1)S(1)}, bf16[4864,1000]{0,1:T(8,128)(2,1)}, u32[]{:S(2)}) copy-start(bf16[4864,1000]{0,1:T(8,128)(2,1)} %copy-done.1) | copy-start | bytes 29184004

commit v2 on v1

--- a/solution.py
+++ b/solution.py
@@ -275,13 +275,60 @@
     )
 
 
+def whiten_body(scale, gram_ref, out_ref, left, right):
+    width = gram_ref.shape[0]
+    eye = lax.broadcasted_iota(jnp.int32, (width, width), 0) == lax.broadcasted_iota(jnp.int32, (width, width), 1)
+    gram = gram_ref[...]
+    diagonal = jnp.where(eye, gram, 0.0)
+    trace = jnp.sum(jnp.sum(diagonal, axis=1, keepdims=True), axis=0, keepdims=True)
+    left[...] = gram + jnp.where(eye, 1e-05 * trace / width, 0.0)
+    right[...] = jnp.where(eye, 1.0, 0.0)
+    place = lax.broadcasted_iota(jnp.int32, (8, width), 0)
+    contract = functools.partial(
+        lax.dot_general,
+        dimension_numbers=(((0,), (0,)), ((), ())),
+        precision=lax.Precision.HIGHEST,
+        preferred_element_type=jnp.float32,
+    )
+
+    def panel(step, carry):
+        rows_left, rows_right = left[:8, :], right[:8, :]
+        columns = [jnp.broadcast_to(rows_left[:, i : i + 1], (8, width)) for i in range(8)]
+        done_left = jnp.zeros((8, width), jnp.float32)
+        done_right = jnp.zeros((8, width), jnp.float32)
+        for i in range(8):
+            inverse = lax.rsqrt(columns[i][i : i + 1, :])
+            top_left, top_right = rows_left[i : i + 1, :] * inverse, rows_right[i : i + 1, :] * inverse
+            done_left = jnp.where(place == i, top_left, done_left)
+            done_right = jnp.where(place == i, top_right, done_right)
+            if i < 7:
+                factor = jnp.where(place > i, columns[i] * inverse, 0.0)
+                rows_left = rows_left - factor * top_left
+                rows_right = rows_right - factor * top_right
+                for j in range(i + 1, 8):
+                    columns[j] = columns[j] - factor * (columns[j][i : i + 1, :] * inverse)
+        out_ref[pl.ds(pl.multiple_of(step * 8, 8), 8), :] = done_right * scale
+        new_left = pltpu.roll(left[...] - contract(done_left, done_left), width - 8, 1)
+        new_right = right[...] - contract(done_left, done_right)
+        left[: width - 8, :] = new_left[8:, :]
+        right[: width - 8, :] = new_right[8:, :]
+        left[width - 8 :, :] = jnp.zeros((8, width), jnp.float32)
+        right[width - 8 :, :] = jnp.zeros((8, width), jnp.float32)
+        return carry
+
+    lax.fori_loop(0, width // 8, panel, 0)
+
+
 def whitening(gram, count):
-    width = gram.shape[0]
-    identity = jnp.eye(width, dtype=jnp.float32)
-    shifted = gram + 1e-05 * jnp.trace(gram) / width * identity
-    lower = jnp.linalg.cholesky(shifted)
-    inverse = jax.scipy.linalg.solve_triangular(lower, identity, lower=True)
-    return jnp.transpose(inverse) * math.sqrt(count)
+    shape = jax.ShapeDtypeStruct(gram.shape, jnp.float32)
+    return pl.pallas_call(
+        functools.partial(whiten_body, math.sqrt(count)),
+        out_shape=shape,
+        in_specs=[pl.BlockSpec(memory_space=pltpu.VMEM)],
+        out_specs=pl.BlockSpec(memory_space=pltpu.VMEM),
+        scratch_shapes=[pltpu.VMEM(gram.shape, jnp.float32)] * 2,
+        compiler_params=pltpu.CompilerParams(vmem_limit_bytes=16 * 1024 * 1024),
+    )(gram)
 
 
 def transposed_product(left, right):
@@ -317,7 +364,13 @@
         part = jnp.dot(resid, omega, preferred_element_type=jnp.float32)
         own = scatter_genes(part, m, ident)
         gram = sum_gram(self_gram(own), n, m, ident + 1)
-        own_basis = jnp.dot(own, whitening(gram, cell_count), precision=lax.Precision.HIGHEST)
+        own_basis = lax.dot_general(
+            own,
+            whitening(gram, cell_count),
+            (((1,), (1,)), ((), ())),
+            precision=lax.Precision.HIGHEST,
+            preferred_element_type=jnp.float32,
+        )
         basis = gather_genes(own_basis.astype(jnp.bfloat16), m, ident + 2)
         partial_sum = transposed_product(resid, basis)
         omega = loading_total(partial_sum, gene_scale, n, ident + 3)

time: 238 us -> 200 us (0.84)
  other arithmetic: 69.4 us -> 22.1 us
  Pallas kernels: 144 us -> 162 us
  matrix products: 21.3 us -> 15.3 us
    another operation x10 -> x0, other arithmetic: 45.7 us -> none  [the longest x6 24.8 us: whitening(): lower = jnp.linalg.cholesky(shifted)]
    pallas_call x0 -> x2, Pallas kernels: none -> 17.8 us  [whitening(): pl.pallas_call(functools.partial(whiten_body, math.sqrt(count)), out_shap...]
    dot_general x2, matrix products: 11.1 us -> 5.52 us  [transposed_product(): lax.dot_general(left, right, (((0,), (0,)), ((), ())), preferred_element_...]
where the time goes in v2:
time: 200 us
  Pallas kernels  162 us (81%)
  other arithmetic  22.1 us (11%)
  matrix products  15.3 us (8%)
    pallas_call x9, Pallas kernels, call(): pl.pallas_call(body, out_shape=out_shape, in_specs=[pl.BlockSpec(memory_s...  144 us
    pallas_call x2, Pallas kernels, whitening(): pl.pallas_call(functools.partial(whiten_body, math.sqrt(count)), out_shap...  17.8 us
    convert_element_type x1, other arithmetic, residual_block(): return jnp.clip(scaled, -limit, limit).astype(jnp.bfloat16)  10.2 us
    reduce_sum x1, other arithmetic, shards(): cell_part = jnp.sum(counts, axis=1).astype(jnp.float32)  8.15 us
    dot_general x2, matrix products, shards(): part = jnp.dot(resid, omega, preferred_element_type=jnp.float32)  5.98 us
    dot_general x2, matrix products, transposed_product(): lax.dot_general(left, right, (((0,), (0,)), ((), ())), preferred_element_...  5.52 us

profile of v2, /device:TPU:0, one launch (start us, length us, event | category | flops | bytes accessed | tf_op | source)
XLA Modules:
  0.0 200.2 jit_solution(11339043551644682157)
XLA Ops:
  0.6 0.0 copy-start
  0.6 8.2 %fusion.6 = (s32[4864]{0:T(1024)S(1)}, s32[1000]{0:T(1024)S(1)}) fusion(s32[4864,1000]{0,1:T(8,128)} %param.2), kind=kLoop, calls=%fused_computation.18 | loop fusion | flops 9722136 | bytes 19479456 | tf_op jit(solution)/shard_map/reduce_sum | solution.py:351
  8.8 11.8 %shard_map.41 = (f32[8,128]{1,0:T(8,128)S(1)}, f32[38,128]{1,0:T(8,128)S(1)}, f32[8,128]{1,0:T(8,128)S(1)}) custom-call(f32[8,128]{1,0:T(8,128)S(1)} %pad_bitcast_fusion.gene_ref, f32[38,128]{1,0:T(8,128)S(1)} %convert_bitcast_fusion.cell_ref), custom_call_target="tpu_custom_call" | custom-call | tf_op jit(solution)/shard_map/pallas_call | solution.py:49
  20.6 0.6 slice_reduce_fusion
  21.2 0.6 slice_divide_fusion
  21.9 10.2 %fusion.2 = bf16[4864,1000]{0,1:T(8,128)(2,1)S(1)} fusion(s32[4864,1000]{0,1:T(8,128)} %param.2, f32[1000]{0:T(1024)S(1)} %slice_divide_fusion, f32[4864]{0:T(1024)S(1)} %bitcast.46), kind=kLoop, calls=%fused_computation.6 | loop fusion | flops 43776000 | bytes 29207456 | tf_op jit(solution)/shard_map/convert_element_type | solution.py:265
  32.0 0.0 copy-done
  32.1 3.0 %fusion.7 = f32[4864,128]{1,0:T(8,128)S(1)} fusion(bf16[4864,1000]{0,1:T(8,128)(2,1)S(1)} %fusion.2, bf16[1000,128]{1,0:T(8,128)(2,1)S(1)} %copy-done), kind=kOutput, calls=%fused_computation.19 | convolution fusion | flops 1245184000 | bytes 12474368 | tf_op jit(solution)/shard_map/dot_general | solution.py:364
  35.1 18.5 %shard_map.42 = f32[1216,128]{1,0:T(8,128)S(1)} custom-call(f32[2,2,1216,128]{3,2,1,0:T(8,128)S(1)} %bitcast.35), custom_call_target="tpu_custom_call" | custom-call | tf_op jit(solution)/shard_map/pallas_call | solution.py:49
  53.6 1.2 fusion.8
  54.8 15.1 %shard_map.43 = f32[8,16,128]{2,1,0:T(8,128)S(1)} custom-call(f32[8,16,128]{2,1,0:T(8,128)S(1)} %bitcast.42), custom_call_target="tpu_custom_call" | custom-call | tf_op jit(solution)/shard_map/pallas_call | solution.py:49
  69.9 9.0 %shard_map.44 = f32[128,128]{1,0:T(8,128)S(1)} custom-call(f32[128,128]{1,0:T(8,128)S(1)} %bitcast.44), custom_call_target="tpu_custom_call" | custom-call | tf_op jit(solution)/shard_map/pallas_call | solution.py:324
  78.9 0.7 convolution_convert_fusion.1.x_ref
  79.6 10.9 %shard_map.45 = bf16[2,2,1216,128]{3,2,1,0:T(8,128)(2,1)S(1)} custom-call(bf16[1216,128]{1,0:T(8,128)(2,1)S(1)} %convolution_convert_fusion.1.x_ref), custom_call_target="tpu_custom_call" | custom-call | tf_op jit(solution)/shard_map/pallas_call | solution.py:49
  90.5 2.8 %fusion.9 = f32[1000,128]{1,0:T(8,128)S(1)} fusion(bf16[4864,1000]{0,1:T(8,128)(2,1)S(1)} %fusion.2, bf16[4864,128]{1,0:T(8,128)(2,1)S(1)} %bitcast.39), kind=kOutput, calls=%fused_computation.21 | convolution fusion | flops 1245184000 | bytes 11485184 | tf_op jit(solution)/shard_map/dot_general | solution.py:335
  93.3 21.8 %shard_map.46 = bf16[8,128,128]{2,1,0:T(8,128)(2,1)S(1)} custom-call(f32[8,128,128]{2,1,0:T(8,128)S(1)} %bitcast.38), custom_call_target="tpu_custom_call" | custom-call | tf_op jit(solution)/shard_map/pallas_call | solution.py:49
  115.1 3.0 %fusion.4 = f32[4864,128]{1,0:T(8,128)S(1)} fusion(bf16[4864,1000]{0,1:T(8,128)(2,1)S(1)} %fusion.2, bf16[1024,128]{1,0:T(8,128)(2,1)S(1)} %bitcast.41), kind=kOutput, calls=%fused_computation.11 | convolution fusion | flops 1245184000 | bytes 12474368 | tf_op jit(solution)/shard_map/dot_general | solution.py:364
  118.1 16.8 %shard_map.47 = f32[1216,128]{1,0:T(8,128)S(1)} custom-call(f32[2,2,1216,128]{3,2,1,0:T(8,128)S(1)} %bitcast.34), custom_call_target="tpu_custom_call" | custom-call | tf_op jit(solution)/shard_map/pallas_call | solution.py:49
  134.8 1.2 fusion.10
  136.1 15.4 %shard_map.48 = f32[8,16,128]{2,1,0:T(8,128)S(1)} custom-call(f32[8,16,128]{2,1,0:T(8,128)S(1)} %bitcast.43), custom_call_target="tpu_custom_call" | custom-call | tf_op jit(solution)/shard_map/pallas_call | solution.py:49
  151.5 8.8 %shard_map.49 = f32[128,128]{1,0:T(8,128)S(1)} custom-call(f32[128,128]{1,0:T(8,128)S(1)} %bitcast.45), custom_call_target="tpu_custom_call" | custom-call | tf_op jit(solution)/shard_map/pallas_call | solution.py:324
  160.3 0.7 convolution_convert_fusion.x_ref
  161.0 9.9 %shard_map.50 = bf16[2,2,1216,128]{3,2,1,0:T(8,128)(2,1)S(1)} custom-call(bf16[1216,128]{1,0:T(8,128)(2,1)S(1)} %convolution_convert_fusion.x_ref), custom_call_target="tpu_custom_call" | custom-call | tf_op jit(solution)/shard_map/pallas_call | solution.py:49
  170.9 2.8 %fusion.11 = f32[1000,128]{1,0:T(8,128)S(1)} fusion(bf16[4864,1000]{0,1:T(8,128)(2,1)S(1)} %fusion.2, bf16[4864,128]{1,0:T(8,128)(2,1)S(1)} %bitcast.36), kind=kOutput, calls=%fused_computation.23 | convolution fusion | flops 1245184000 | bytes 11485184 | tf_op jit(solution)/shard_map/dot_general | solution.py:335
  173.7 23.9 %shard_map.51 = bf16[8,128,128]{2,1,0:T(8,128)(2,1)S(1)} custom-call(f32[8,128,128]{2,1,0:T(8,128)S(1)} %bitcast.37), custom_call_target="tpu_custom_call" | custom-call | tf_op jit(solution)/shard_map/pallas_call | solution.py:49
  197.6 0.8 slice_convert_fusion
  198.5 1.7 bitcast_convert_fusion
  (5 shorter events, 0.1 us)
Async XLA Ops:
  0.6 31.4 %copy-start = (bf16[1000,128]{1,0:T(8,128)(2,1)S(1)}, bf16[1000,128]{1,0:T(8,128)(2,1)}, u32[]{:S(2)}) copy-start(bf16[1000,128]{1,0:T(8,128)(2,1)} %param.3) | copy-start | bytes 768004
